TPU v7x, 256 devices: a 8x8x2 block of a 8x8x16 slice. The times are simulated.
256 devices in a mesh: groups: 2 (over z), pre: 16 (over y, core), dec: 8 (over x).
Axes of the slice: x: 8, y: 8, z: 2, core: 2. Of those that a mesh axis runs over, the one named last changes fastest.
The devices are a block of a 8x8x16 slice.
Arguments:
- tokens: bfloat16 [32768, 2048], P(('groups', 'pre', 'dec')), parts along dimension 0, may hold values from -6 to 6
- attended: bfloat16 [32768, 2048], P(('groups', 'pre', 'dec')), parts along dimension 0, may hold values from -6 to 6
- input_gain: float32 [2048], replicated, may hold values from 0.25 to 1.75
- post_gain: float32 [2048], replicated, may hold values from 0.25 to 1.75
- kv_weight: bfloat16 [2048, 1024], P('pre'), may hold values from -0.125 to 0.125
- key_gain: float32 [128], replicated, may hold values from 0.25 to 1.75
- w_gate: bfloat16 [128, 2048, 768], P(('pre', 'dec')), may hold values from -0.125 to 0.125
- w_up: bfloat16 [128, 2048, 768], P(('pre', 'dec')), may hold values from -0.125 to 0.125
- w_down: bfloat16 [128, 768, 2048], P(('pre', 'dec')), may hold values from -0.21875 to 0.21875
- expert_ids: int32 [32768, 8], P(('groups', 'pre', 'dec')), parts along dimension 0, may hold values from 0 to 127, all different within a row; in each aligned block of 128 rows (0 to 127, 128 to 255, ...) at most 10 rows name the same one
- gate_weights: float32 [32768, 8], P(('groups', 'pre', 'dec')), parts along dimension 0, may hold values from 0.05 to 1
- page_list: int32 [32, 64], P(('groups', 'pre')), parts along dimension 0, may hold values from 0 to 63, each once within a row
- lengths: int32 [32, 8], P(('groups', 'pre')), parts along dimension 0, may hold values from 1 to 16, 64 in all within a row
- assignment: int32 [256, 1], P(('groups', 'pre')), parts along dimension 0, may hold values from 0 to 7; in each aligned block of 8 rows (0 to 7, 8 to 15, ...) at most 3 rows name the same one
- query: bfloat16 [256, 4096], P(('groups', 'pre')), parts along dimension 0, may hold values from -300 to 300
- new_kv: bfloat16 [256, 1024], P(('groups', 'pre')), parts along dimension 0, may hold values from -6 to 6
Outputs:
- moe_out: bfloat16 [32768, 2048], P(('groups', 'pre', 'dec')), parts along dimension 0
- decode_out: bfloat16 [768, 4096], P(('groups', 'pre', 'dec')), parts along dimension 0
There are 2 independent parts, one for each index of `groups`. A program takes and returns all parts, laid end to end along the dimension named above; an argument that names none is the same for every part. Nothing has to cross between parts.
Inputs may be any that keep to these rules, and one draw needn't show every extreme that they name: `expert_ids`: each row names 8 different experts; among the rows of one device no expert is named by more than 10 rows, and some expert reaches 10. `page_list`: each slab's row names each of its pages once. Each slab's lengths sum to 64. `assignment`: within each aligned block of 8 requests (one slab) no decoding device is named more than 3 times, and some block reaches 3.
All inputs are finite; a program needn't handle non-finite values.
Results may differ from a plain program's by a relative error of at most 0.0055.
The roundings to bfloat16 on the way count: a program that leaves them out, or rounds other values in their place, can miss the bound.
Values may be sent and summed in bfloat16 or wider, within the bound.
A program may use at most 128 MiB of HBM per device.

v0:
```python
import jax
import jax.numpy as jnp
from jax import lax
from jax.sharding import PartitionSpec as P

H = 32
KVH = 4
HD = 128
PAGE = 16
RCAP = 3


EPSILON = 1e-06
FLOOR_SCORE = -1e30


def grouped_exchange(shard, axis, split_dim, concat_dim, work, item_dim, out_dim):

    def moved(group):
        return lax.all_to_all(group, axis, split_axis=split_dim, concat_axis=concat_dim, tiled=True)

    items = jax.tree.leaves(shard)[0].shape[item_dim]
    ends = [items * k // 2 for k in range(2 + 1)] if items % 2 == 0 else [0, items]
    groups = [
        jax.tree.map(lambda a: lax.slice_in_dim(a, low, high, axis=item_dim), shard)
        for low, high in zip(ends, ends[1:])
    ]
    arrived = [moved(group) for group in groups]
    made = [work(group) for group in arrived]
    return jax.tree.map(lambda *parts: jnp.concatenate(parts, axis=out_dim), *made)


def all_in_one(shard, axis):
    leaves = jax.tree.leaves(shard)
    sequence = sorted(range(len(leaves)), key=lambda k: -leaves[k].size)
    width = (1, *leaves[sequence[0]].shape)[-1]
    lines = [
        jnp.pad(leaves[k].reshape(-1), (0, -leaves[k].size % width)).reshape(-1, width)
        for k in sequence
    ]
    both, at, found = (lax.all_gather(jnp.concatenate(lines), axis), 0, {})
    for k, line in zip(sequence, lines):
        section = both[:, at : at + len(line)].reshape(len(both), -1)
        found[k] = section[:, : leaves[k].size].reshape(-1, *leaves[k].shape)
        at += len(line)
    numbers = iter(range(len(leaves)))
    return jax.tree.map(lambda _: found[next(numbers)], shard)


def joined(part, axis, combine):
    gathered = all_in_one(part, axis)

    def take(source):
        return jax.tree.map(lambda a: lax.dynamic_index_in_dim(a, source, 0, False), gathered)

    return lax.fori_loop(
        1, lax.axis_size(axis), lambda source, state: combine(state, take(source)), take(0)
    )


def norm_rows(values, scales):
    values = values.astype(jnp.float32)
    factor = lax.rsqrt(jnp.mean(values * values, axis=-1, keepdims=True) + EPSILON)
    return values * factor * scales


def token_requests(page_order, page_counts):
    page_total = page_order.shape[0]
    request_ends = jnp.cumsum(page_counts)
    positions = jnp.arange(page_total, dtype=jnp.int32)
    owner_at = jnp.sum((positions[:, None] >= request_ends[None, :]).astype(jnp.int32), axis=1)
    matches = page_order[:, None] == positions[None, :]
    page_owner = jnp.sum(jnp.where(matches, owner_at[:, None], 0), axis=0)
    return jnp.repeat(page_owner, PAGE)


def slot_requests(owners, device, slot_count):
    request_count = owners.shape[0]
    is_mine = (owners == device).astype(jnp.int32)
    order_mine = jnp.cumsum(is_mine) - 1
    slot_hit = (is_mine[None, :] == 1) & (
        order_mine[None, :] == jnp.arange(slot_count, dtype=jnp.int32)[:, None]
    )
    targets = jnp.sum(
        jnp.where(slot_hit, jnp.arange(request_count, dtype=jnp.int32)[None, :], 0), axis=1
    )
    return (targets, jnp.any(slot_hit, axis=1))


def empty_state(count):
    group = H // KVH
    return (
        jnp.full((count, KVH, group), FLOOR_SCORE, jnp.float32),
        jnp.zeros((count, KVH, group), jnp.float32),
        jnp.zeros((count, KVH, group, HD), jnp.float32),
    )


def attend_block(state, queries, targets, live, piece, piece_owner):
    peak, total, mixed = state
    row_count = piece.shape[0]
    half = KVH * HD
    piece_keys = piece[:, :half].reshape(row_count, KVH, HD)
    piece_values = piece[:, half:].reshape(row_count, KVH, HD).astype(jnp.float32)
    scores = jnp.einsum(
        "skgd,tkd->skgt", queries, piece_keys, preferred_element_type=jnp.float32
    ) * HD ** (-0.5)
    members = ((piece_owner[None, :] == targets[:, None]) & live[:, None])[:, None, None, :]
    scores = jnp.where(members, scores, FLOOR_SCORE)
    raised = jnp.maximum(peak, jnp.max(scores, axis=-1))
    weights = jnp.where(members, jnp.exp(scores - raised[..., None]), 0.0)
    total = jnp.sum(weights, axis=-1)
    mixed = jnp.einsum("skgt,tkd->skgd", weights, piece_values, precision=lax.Precision.HIGHEST)
    return (raised, total, mixed)


def join(first, second):
    highest = jnp.maximum(first[0], second[0])
    first_part = jnp.exp(first[0] - highest)
    second_part = jnp.exp(second[0] - highest)
    return (
        highest,
        first[1] * first_part + second[1] * second_part,
        first[2] * first_part[..., None] + second[2] * second_part[..., None],
    )


def finish(state, queries, fresh):
    peak, total, mixed = state
    count = queries.shape[0]
    half = KVH * HD
    new_keys = fresh[:, :half].reshape(count, KVH, HD)
    new_values = fresh[:, half:].reshape(count, KVH, HD).astype(jnp.float32)
    own_score = jnp.einsum(
        "skgd,skd->skg", queries, new_keys, preferred_element_type=jnp.float32
    ) * HD ** (-0.5)
    highest = jnp.maximum(peak, own_score)
    old_part = jnp.exp(peak - highest)
    new_part = jnp.exp(own_score - highest)
    mixed = mixed * old_part[..., None] + new_part[..., None] * new_values[:, :, None, :]
    return (mixed / (total * old_part + new_part)[..., None]).reshape(count, H * HD)


def body(
    tokens,
    attended,
    input_gain,
    post_gain,
    kv_weight,
    key_gain,
    w_gate,
    w_up,
    w_down,
    expert_ids,
    gate_weights,
    page_list,
    lengths,
    assignment,
    query,
    new_kv,
):
    local_tokens = tokens.shape[0]
    model_width = tokens.shape[1]
    normed_in = norm_rows(tokens, input_gain).astype(jnp.bfloat16)
    projected = jnp.dot(
        normed_in,
        lax.all_gather(kv_weight, "pre", axis=0, tiled=True),
        preferred_element_type=jnp.float32,
    )
    half = KVH * HD
    keys = norm_rows(projected[:, :half].reshape(local_tokens, KVH, HD), key_gain).astype(
        jnp.bfloat16
    )
    cache = jnp.concatenate(
        [keys.reshape(local_tokens, half), projected[:, half:].astype(jnp.bfloat16)], axis=1
    )
    normed = norm_rows(attended, post_gain).astype(jnp.bfloat16)
    experts_here = w_gate.shape[0]
    pre_count = lax.axis_size("pre")
    experts_all = experts_here * pre_count * lax.axis_size("dec")
    top_count = expert_ids.shape[1]
    capacity = max(2, local_tokens * top_count * 5 // (4 * experts_all))
    flat_ids = expert_ids.reshape(-1)
    picks = (flat_ids[:, None] == jnp.arange(experts_all, dtype=jnp.int32)[None, :]).astype(
        jnp.int32
    )
    before = jnp.sum((jnp.cumsum(picks, axis=0) - 1) * picks, axis=1)
    slot_index = flat_ids * capacity + before
    source_rows = jnp.repeat(jnp.arange(local_tokens, dtype=jnp.int32), top_count)
    outgoing = (
        jnp.zeros((experts_all * capacity, model_width), jnp.bfloat16)
        .at[slot_index]
        .set(normed[source_rows])
    )

    def run_experts(received):
        count = received.shape[1]
        grouped = received.reshape(-1, experts_here, count, model_width)
        gate_part = jnp.einsum(
            "necd,edf->necf", grouped, w_gate, preferred_element_type=jnp.float32
        )
        up_part = jnp.einsum("necd,edf->necf", grouped, w_up, preferred_element_type=jnp.float32)
        hidden = (jax.nn.silu(gate_part) * up_part).astype(jnp.bfloat16)
        result = jnp.einsum(
            "necf,efd->necd", hidden, w_down, preferred_element_type=jnp.float32
        ).astype(jnp.bfloat16)
        return result.reshape(-1, count, model_width)

    def serve(received):
        return lax.all_to_all(
            run_experts(received), ("pre", "dec"), split_axis=0, concat_axis=0, tiled=True
        )

    returned = grouped_exchange(
        outgoing.reshape(experts_all, capacity, model_width), ("pre", "dec"), 0, 0, serve, 1, 1
    )
    rows_back = returned.reshape(experts_all * capacity, model_width)
    picked = rows_back[slot_index].reshape(local_tokens, top_count, model_width).astype(jnp.float32)
    route = gate_weights / jnp.sum(gate_weights, axis=-1, keepdims=True)
    moe_out = jnp.einsum("tk,tkd->td", route, picked, precision=lax.Precision.HIGHEST).astype(
        jnp.bfloat16
    )
    device = lax.axis_index("dec")
    owners = assignment[:, 0]
    request_count = owners.shape[0]
    owner_of = token_requests(page_list[0], lengths[0])
    targets, live = slot_requests(owners, device, RCAP)
    group = H // KVH
    everyone = query.reshape(request_count, KVH, group, HD)
    local_owner = lax.dynamic_slice_in_dim(owner_of, device * local_tokens, local_tokens, 0)
    partial_state = attend_block(
        empty_state(request_count),
        everyone,
        jnp.arange(request_count, dtype=jnp.int32),
        jnp.ones((request_count,), jnp.bool_),
        cache,
        local_owner,
    )
    state = joined(partial_state, "dec", join)
    request_rows = finish(state, everyone, new_kv).astype(jnp.bfloat16)
    decode_out = jnp.where(live[:, None], request_rows[targets], jnp.zeros((), jnp.bfloat16))
    return (moe_out, decode_out)


def solution(mesh):
    in_specs = (
        P(("groups", "pre", "dec"), None),
        P(("groups", "pre", "dec"), None),
        P(),
        P(),
        P("pre", None),
        P(),
        P(("pre", "dec"), None, None),
        P(("pre", "dec"), None, None),
        P(("pre", "dec"), None, None),
        P(("groups", "pre", "dec"), None),
        P(("groups", "pre", "dec"), None),
        P(("groups", "pre"), None),
        P(("groups", "pre"), None),
        P(("groups", "pre"), None),
        P(("groups", "pre"), None),
        P(("groups", "pre"), None),
    )
    out_specs = (P(("groups", "pre", "dec"), None), P(("groups", "pre", "dec"), None))
    return jax.shard_map(body, mesh=mesh, in_specs=in_specs, out_specs=out_specs, check_vma=False)
```

profile of v0, /device:TPU:520, one launch (start us, length us, event | category | flops | bytes accessed | tf_op | source)
XLA Modules:
  0.0 594.5 jit_solution(6112036630714619702)
XLA Ops:
  7.2 0.9 copy.90
  8.3 0.7 broadcast_multiply_fusion
  9.3 0.8 copy-done.2
  10.2 1.1 add_add_fusion
  11.2 0.9 copy.93
  12.3 1.2 fusion.54
  13.7 1.4 fusion.64
  15.2 2.0 fusion.56
  17.2 23.6 %scatter_custom_fusion = bf16[1280,2048]{1,0:T(8,128)(2,1)} fusion(s32[1024]{0:T(1024)S(1)} %bitcast.192, bf16[128,2048]{1,0:T(8,128)(2,1)} %fusion.56, s32[1024]{0:T(1024)S(1)} %broadcast_clamp_fusion.1, bf16[]{:T(256)} %constant.96.clone.1), kind=kCustom, calls=%fused_computation.15 | custom fusion | bytes 5243392 | tf_op jit(solution)/shard_map/scatter | solution.py:193
  40.8 9.5 %reshape.307 = bf16[128,10,2048]{2,1,0:T(8,128)(2,1)} reshape(bf16[1280,2048]{1,0:T(8,128)(2,1)} %scatter_custom_fusion) | data formatting | bytes 10485760 | tf_op jit(solution)/shard_map/reshape | solution.py:215
  50.4 7.7 %fusion.93 = (bf16[128,5,2048]{2,1,0:T(8,128)(2,1)}, bf16[128,5,2048]{2,1,0:T(8,128)(2,1)}) fusion(bf16[128,10,2048]{2,1,0:T(8,128)(2,1)} %reshape.307), kind=kLoop, calls=%fused_computation.134 | loop fusion | bytes 10485760 | tf_op jit(solution)/shard_map/slice | solution.py:25
  58.1 26.7 %all-to-all-start = ((bf16[128,5,2048]{2,1,0:T(8,128)(2,1)}), bf16[128,5,2048]{2,1,0:T(8,128)(2,1)}, u32[]{:S(2)}, u32[]{:S(2)}) async-start(bf16[128,5,2048]{2,1,0:T(8,128)(2,1)} %get-tuple-element.206), calls=%async_computation | async-start | bytes 8388608 | tf_op jit(solution)/shard_map/all_to_all | solution.py:20
  84.9 0.7 all-gather.5.cloned.1.call-update
  85.6 106.2 %all-to-all-done = bf16[128,5,2048]{2,1,0:T(8,128)(2,1)} async-done(((bf16[128,5,2048]{2,1,0:T(8,128)(2,1)}), bf16[128,5,2048]{2,1,0:T(8,128)(2,1)}, u32[]{:S(2)}, u32[]{:S(2)}) %all-to-all-start) | async-done | bytes 2621472 | tf_op jit(solution)/shard_map/all_to_all | solution.py:20
  191.8 14.3 %all-to-all-start.2 = ((bf16[128,5,2048]{2,1,0:T(8,128)(2,1)}), bf16[128,5,2048]{2,1,0:T(8,128)(2,1)}, u32[]{:S(2)}, u32[]{:S(2)}) async-start(bf16[128,5,2048]{2,1,0:T(8,128)(2,1)} %get-tuple-element.207), calls=%async_computation.2 | async-start | bytes 8388608 | tf_op jit(solution)/shard_map/all_to_all | solution.py:20
  206.9 0.7 copy.109
  207.7 9.1 %fusion.15 = f32[128,5,768]{2,0,1:T(8,128)} fusion(bf16[1,2048,768]{2,1,0:T(8,128)(2,1)} %param.24, bf16[128,5,2048]{2,1,0:T(8,128)(2,1)} %all-to-all-done), kind=kOutput, calls=%fused_computation.27 | convolution fusion | flops 2013265920 | bytes 7733248 | tf_op jit(solution)/shard_map/necd,edf->necf/dot_general | solution.py:199
  216.7 12.0 %convolution_convert_fusion.1 = bf16[128,5,2048]{2,0,1:T(8,128)(2,1)} fusion(bf16[1,768,2048]{2,1,0:T(8,128)(2,1)S(1)} %copy-done, bf16[1,2048,768]{2,1,0:T(8,128)(2,1)} %param.25, bf16[128,5,2048]{2,1,0:T(8,128)(2,1)} %all-to-all-done, f32[128,5,768]{2,0,1:T(8,128)} %fusion.15), kind=kOutput, calls=%fused_computation.18 | convolution fusion | flops 4030791680 | bytes 13500416 | tf_op jit(solution)/shard_map/necf,efd->necd/dot_general | solution.py:204
  228.7 5.4 copy.96
  234.1 75.7 %all-to-all-done.2 = bf16[128,5,2048]{2,1,0:T(8,128)(2,1)} async-done(((bf16[128,5,2048]{2,1,0:T(8,128)(2,1)}), bf16[128,5,2048]{2,1,0:T(8,128)(2,1)}, u32[]{:S(2)}, u32[]{:S(2)}) %all-to-all-start.2) | async-done | bytes 2621472 | tf_op jit(solution)/shard_map/all_to_all | solution.py:20
  309.8 13.6 %all-to-all-start.1 = ((bf16[128,5,2048]{2,1,0:T(8,128)(2,1)}), bf16[128,5,2048]{2,1,0:T(8,128)(2,1)}, u32[]{:S(2)}, u32[]{:S(2)}) async-start(bf16[128,5,2048]{2,1,0:T(8,128)(2,1)} %copy.96), calls=%async_computation.1 | async-start | bytes 8388608 | tf_op jit(solution)/shard_map/all_to_all | solution.py:210
  325.0 1.2 fusion.57
  326.8 0.8 fusion.77
  327.6 3.1 fusion.62
  330.7 0.7 slice.65
  331.4 1.0 reshape.319
  333.4 0.9 fusion.70
  334.3 1.1 fusion.96
  335.4 1.2 convolution_bitcast_fusion
  336.7 0.9 fusion.73
  338.5 9.1 %fusion.13 = f32[128,5,768]{2,0,1:T(8,128)} fusion(bf16[1,2048,768]{2,1,0:T(8,128)(2,1)} %param.24, bf16[128,5,2048]{2,1,0:T(8,128)(2,1)} %all-to-all-done.2), kind=kOutput, calls=%fused_computation.25 | convolution fusion | flops 2013265920 | bytes 7733248 | tf_op jit(solution)/shard_map/necd,edf->necf/dot_general | solution.py:199
  347.5 12.2 %convolution_convert_fusion = bf16[128,5,2048]{2,0,1:T(8,128)(2,1)} fusion(bf16[1,768,2048]{2,1,0:T(8,128)(2,1)S(1)} %copy-done, bf16[1,2048,768]{2,1,0:T(8,128)(2,1)} %param.25, bf16[128,5,2048]{2,1,0:T(8,128)(2,1)} %all-to-all-done.2, f32[128,5,768]{2,0,1:T(8,128)} %fusion.13), kind=kOutput, calls=%fused_computation.17 | convolution fusion | flops 4030791680 | bytes 13500416 | tf_op jit(solution)/shard_map/necf,efd->necd/dot_general | solution.py:204
  359.8 5.2 copy.99
  364.9 67.0 %all-to-all-done.1 = bf16[128,5,2048]{2,1,0:T(8,128)(2,1)} async-done(((bf16[128,5,2048]{2,1,0:T(8,128)(2,1)}), bf16[128,5,2048]{2,1,0:T(8,128)(2,1)}, u32[]{:S(2)}, u32[]{:S(2)}) %all-to-all-start.1) | async-done | bytes 2621472 | tf_op jit(solution)/shard_map/all_to_all | solution.py:210
  431.9 10.5 %all-to-all-start.3 = ((bf16[128,5,2048]{2,1,0:T(8,128)(2,1)}), bf16[128,5,2048]{2,1,0:T(8,128)(2,1)}, u32[]{:S(2)}, u32[]{:S(2)}) async-start(bf16[128,5,2048]{2,1,0:T(8,128)(2,1)} %copy.99), calls=%async_computation.3 | async-start | bytes 8388608 | tf_op jit(solution)/shard_map/all_to_all | solution.py:210
  442.4 0.8 fusion.94
  443.7 0.8 fusion.95
  444.6 1.3 slice.68
  446.0 0.9 dynamic_slice.50
  446.9 1.6 while.19
  448.7 0.7 gather_fusion.1
  449.5 0.7 broadcast_select_fusion
  450.2 97.9 %all-to-all-done.3 = bf16[128,5,2048]{2,1,0:T(8,128)(2,1)} async-done(((bf16[128,5,2048]{2,1,0:T(8,128)(2,1)}), bf16[128,5,2048]{2,1,0:T(8,128)(2,1)}, u32[]{:S(2)}, u32[]{:S(2)}) %all-to-all-start.3) | async-done | bytes 2621472 | tf_op jit(solution)/shard_map/all_to_all | solution.py:210
  548.0 10.4 %pad_maximum_fusion = bf16[128,10,2048]{2,1,0:T(8,128)(2,1)} fusion(bf16[128,5,2048]{2,1,0:T(8,128)(2,1)} %all-to-all-done.3, bf16[128,5,2048]{2,1,0:T(8,128)(2,1)} %all-to-all-done.1), kind=kLoop, calls=%fused_computation.12 | loop fusion | flops 10485760 | bytes 10485760 | tf_op jit(solution)/shard_map/concatenate | solution.py:30
  558.5 9.8 %reshape.313 = bf16[1280,2048]{1,0:T(8,128)(2,1)} reshape(bf16[128,10,2048]{2,1,0:T(8,128)(2,1)} %pad_maximum_fusion) | data formatting | bytes 10485760 | tf_op jit(solution)/shard_map/reshape | solution.py:217
  568.3 12.1 %gather_fusion = bf16[1024,2048]{1,0:T(8,128)(2,1)} fusion(bf16[1280,2048]{1,0:T(8,128)(2,1)} %reshape.313, s32[1024]{0:T(1024)S(1)} %broadcast_clamp_fusion), kind=kCustom, calls=%fused_computation.1 | custom fusion | bytes 8392704 | tf_op jit(solution)/shard_map/gather | solution.py:218
  580.5 5.7 fusion.3
  586.2 1.1 copy.154
  (103 shorter events, 8.0 us)
Async XLA Ops:
  7.2 209.6 %copy-start = (bf16[1,768,2048]{2,1,0:T(8,128)(2,1)S(1)}, bf16[1,768,2048]{2,1,0:T(8,128)(2,1)}, u32[]{:S(2)}) copy-start(bf16[1,768,2048]{2,1,0:T(8,128)(2,1)} %param.26) | copy-start | bytes 9437188
  7.2 7.9 %copy-start.9 = (f32[2048]{0:T(1024)S(1)}, f32[2048]{0:T(1024)}, u32[]{:S(2)}) copy-start(f32[2048]{0:T(1024)} %param.21) | copy-start | bytes 24580
  9.3 0.8 copy-start.2
  15.1 25.7 %copy-start.4 = (s32[1024,1]{0,1:T(1,128)}, s32[1024,1]{0,1:T(1,128)S(1)}, u32[]{:S(2)}) copy-start(s32[1024,1]{0,1:T(1,128)S(1)} %compare_select_fusion.1) | copy-start | bytes 12292
  58.1 133.7 %all-to-all-start = ((bf16[128,5,2048]{2,1,0:T(8,128)(2,1)}), bf16[128,5,2048]{2,1,0:T(8,128)(2,1)}, u32[]{:S(2)}, u32[]{:S(2)}) async-start(bf16[128,5,2048]{2,1,0:T(8,128)(2,1)} %get-tuple-element.206), calls=%async_computation | async-start | bytes 8388608 | tf_op jit(solution)/shard_map/all_to_all | solution.py:20
  84.8 242.8 %all-gather.5.cloned.1.call-start = ((), (), s32[]{:S(2)}) async-start(), calls=%async_computation.4 | async-start | bytes 4456448 | tf_op jit(solution)/shard_map/all_gather | solution.py:167
  191.8 14.3 %copy-start.14 = (s32[1,8]{1,0:T(1,128)S(1)}, s32[1,8]{1,0:T(1,128)}, u32[]{:S(2)}) copy-start(s32[1,8]{1,0:T(1,128)} %param.30) | copy-start | bytes 100
  191.8 14.6 %copy-start.15 = (s32[1,64]{1,0:T(1,128)S(1)}, s32[1,64]{1,0:T(1,128)}, u32[]{:S(2)}) copy-start(s32[1,64]{1,0:T(1,128)} %param.29) | copy-start | bytes 772
  191.8 14.8 %copy-start.7 = (bf16[8,1024]{1,0:T(8,128)(2,1)S(1)}, bf16[8,1024]{1,0:T(8,128)(2,1)}, u32[]{:S(2)}) copy-start(bf16[8,1024]{1,0:T(8,128)(2,1)} %param.33) | copy-start | bytes 49156
  191.8 14.9 %copy-start.12 = (s32[8,1]{0,1:T(1,128)S(1)}, s32[8,1]{0,1:T(1,128)}, u32[]{:S(2)}) copy-start(s32[8,1]{0,1:T(1,128)} %param.31) | copy-start | bytes 100
  191.8 15.1 %copy-start.6 = (f32[128,8]{0,1:T(8,128)S(1)}, f32[128,8]{0,1:T(8,128)}, u32[]{:S(2)}) copy-start(f32[128,8]{0,1:T(8,128)} %param.28) | copy-start | bytes 12292
  191.8 118.0 %all-to-all-start.2 = ((bf16[128,5,2048]{2,1,0:T(8,128)(2,1)}), bf16[128,5,2048]{2,1,0:T(8,128)(2,1)}, u32[]{:S(2)}, u32[]{:S(2)}) async-start(bf16[128,5,2048]{2,1,0:T(8,128)(2,1)} %get-tuple-element.207), calls=%async_computation.2 | async-start | bytes 8388608 | tf_op jit(solution)/shard_map/all_to_all | solution.py:20
  234.1 92.7 %copy-start.13 = (bf16[8,4096]{1,0:T(8,128)(2,1)S(1)}, bf16[8,4096]{1,0:T(8,128)(2,1)}, u32[]{:S(2)}) copy-start(bf16[8,4096]{1,0:T(8,128)(2,1)} %param.32) | copy-start | bytes 196612
  234.1 93.5 %copy-start.10 = (f32[2048]{0:T(1024)S(1)}, f32[2048]{0:T(1024)}, u32[]{:S(2)}) copy-start(f32[2048]{0:T(1024)} %param.20) | copy-start | bytes 24580
  309.8 122.1 %all-to-all-start.1 = ((bf16[128,5,2048]{2,1,0:T(8,128)(2,1)}), bf16[128,5,2048]{2,1,0:T(8,128)(2,1)}, u32[]{:S(2)}, u32[]{:S(2)}) async-start(bf16[128,5,2048]{2,1,0:T(8,128)(2,1)} %copy.96), calls=%async_computation.1 | async-start | bytes 8388608 | tf_op jit(solution)/shard_map/all_to_all | solution.py:210
  323.5 118.9 %all-gather.7.cloned.1.call-start = ((), (), s32[]{:S(2)}) async-start(), calls=%async_computation.5 | async-start | bytes 1216512 | tf_op jit(solution)/shard_map/all_gather | solution.py:41
  364.9 77.4 %copy-start.5 = (s32[1024,1]{0,1:T(1,128)S(1)}, s32[1024,1]{0,1:T(1,128)}, u32[]{:S(2)}) copy-start(s32[1024,1]{0,1:T(1,128)} %copy-done.4) | copy-start | bytes 12292
  431.9 116.1 %all-to-all-start.3 = ((bf16[128,5,2048]{2,1,0:T(8,128)(2,1)}), bf16[128,5,2048]{2,1,0:T(8,128)(2,1)}, u32[]{:S(2)}, u32[]{:S(2)}) async-start(bf16[128,5,2048]{2,1,0:T(8,128)(2,1)} %copy.99), calls=%async_computation.3 | async-start | bytes 8388608 | tf_op jit(solution)/shard_map/all_to_all | solution.py:210
  442.4 6.1 %copy-start.8 = (f32[8,4,1,8]{3,2,1,0:T(1,128)S(1)}, f32[8,4,1,8]{3,2,1,0:T(1,128)}, u32[]{:S(2)}) copy-start(f32[8,4,1,8]{3,2,1,0:T(1,128)} %fusion.77) | copy-start | bytes 3076
  443.7 5.8 copy-start.11
  568.3 12.1 %copy-start.3 = (f32[128,8,1]{1,2,0:T(1,128)S(1)}, f32[128,8,1]{1,2,0:T(1,128)}, u32[]{:S(2)}) copy-start(f32[128,8,1]{1,2,0:T(1,128)} %copy.109) | copy-start | bytes 12292
  568.3 19.0 %copy-start.1 = (bf16[1,768,2048]{2,1,0:T(8,128)(2,1)S(1)}, bf16[1,768,2048]{2,1,0:T(8,128)(2,1)}, u32[]{:S(2)}) copy-start(bf16[1,768,2048]{2,1,0:T(8,128)(2,1)} %param.26) | copy-start | bytes 9437188
Sparse Core Ops, SparseCore 0:
  87.5 118.9 all-gather.4
  338.6 59.7 all-gather.6
where the time goes:
time: 604 us; the launch traced here: 595 us
  waiting for transfers between devices  348 us (58%)
  local copies, waits for them, and re-layouts  86.5 us (14%)
  starting transfers between devices  65.2 us (11%)
  matrix products  54.3 us (9%)
  other arithmetic  25.9 us (4%)
  between operations  14.9 us (2%)
    all_to_all x2, waiting for transfers between devices, moved(): lax.all_to_all(group, axis, split_axis=split_dim, concat_axis=concat_dim,...  182 us
    all_to_all x2, waiting for transfers between devices, serve(): lax.all_to_all(run_experts(received), ('pre', 'dec'), split_axis=0, conca...  165 us
    all_to_all x2, starting transfers between devices, moved(): lax.all_to_all(group, axis, split_axis=split_dim, concat_axis=concat_dim,...  41 us
    dot_general x2, matrix products, run_experts(): jnp.einsum('necf,efd->necd', hidden, w_down, preferred_element_type=jnp.f...  24.2 us
    all_to_all x2, starting transfers between devices, serve(): lax.all_to_all(run_experts(received), ('pre', 'dec'), split_axis=0, conca...  24.1 us
    scatter x1, local copies, waits for them, and re-layouts, body(): outgoing = jnp.zeros((experts_all * capacity, model_width), jnp.bfloat16)...  23.6 us
    dot_general x2, matrix products, run_experts(): jnp.einsum('necd,edf->necf', grouped, w_gate, preferred_element_type=jnp....  18.1 us
    gather x1, local copies, waits for them, and re-layouts, body(): rows_back[slot_index].reshape(local_tokens, top_count, model_width)  12.1 us
  transfers between devices with their start and end apart: 6, of which 4 were waited for; matrix products, arithmetic and copies ran while one was open for 13% of the time, Pallas kernels for 0%

commit v1 on v0

--- a/solution.py
+++ b/solution.py
@@ -1,7 +1,13 @@
+import functools
+
 import jax
 import jax.numpy as jnp
 from jax import lax
+from jax.experimental import pallas as pl
+from jax.experimental.pallas import tpu as pltpu
 from jax.sharding import PartitionSpec as P
+
+MESH = pl.DeviceIdType.MESH
 
 H = 32
 KVH = 4
@@ -12,22 +18,6 @@
 
 EPSILON = 1e-06
 FLOOR_SCORE = -1e30
-
-
-def grouped_exchange(shard, axis, split_dim, concat_dim, work, item_dim, out_dim):
-
-    def moved(group):
-        return lax.all_to_all(group, axis, split_axis=split_dim, concat_axis=concat_dim, tiled=True)
-
-    items = jax.tree.leaves(shard)[0].shape[item_dim]
-    ends = [items * k // 2 for k in range(2 + 1)] if items % 2 == 0 else [0, items]
-    groups = [
-        jax.tree.map(lambda a: lax.slice_in_dim(a, low, high, axis=item_dim), shard)
-        for low, high in zip(ends, ends[1:])
-    ]
-    arrived = [moved(group) for group in groups]
-    made = [work(group) for group in arrived]
-    return jax.tree.map(lambda *parts: jnp.concatenate(parts, axis=out_dim), *made)
 
 
 def all_in_one(shard, axis):
@@ -139,6 +129,448 @@
     new_part = jnp.exp(own_score - highest)
     mixed = mixed * old_part[..., None] + new_part[..., None] * new_values[:, :, None, :]
     return (mixed / (total * old_part + new_part)[..., None]).reshape(count, H * HD)
+
+
+def moe_kernel(
+    n,
+    cap,
+    att,
+    gain,
+    meta,
+    wg_hbm,
+    wu_hbm,
+    wd_hbm,
+    out,
+    wg,
+    wu,
+    wd,
+    gathered,
+    metas,
+    keys,
+    routes,
+    outbox,
+    inbox,
+    hidden,
+    results,
+    combined,
+    mix,
+    tall,
+    part,
+    ring_out,
+    ring_in,
+    w_sem,
+    ag_send,
+    ag_recv,
+    meta_send,
+    meta_recv,
+    out_send,
+    out_recv,
+    back_send,
+    back_recv,
+    rs_send,
+    rs_recv,
+):
+    rows, width = att.shape
+    top = meta.shape[0] // 2
+    block = n * cap
+    half_rows = rows // 2
+    far = n // 2
+    g, pre, x = lax.axis_index("groups"), lax.axis_index("pre"), lax.axis_index("dec")
+    y, c = lax.div(pre, 2), lax.rem(pre, 2)
+    f = x * (1 - c) + y * c
+    s = y * (1 - c) + x * c
+
+    def device(first, second, core, orient):
+        first, second = lax.rem(first + 2 * n, n), lax.rem(second + 2 * n, n)
+        at_x = first * (1 - orient) + second * orient
+        at_y = second * (1 - orient) + first * orient
+        return (g, at_y * 2 + core, at_x)
+
+    def remote(source, target, send, recv, where):
+        return pltpu.make_async_remote_copy(
+            src_ref=source,
+            dst_ref=target,
+            send_sem=send,
+            recv_sem=recv,
+            device_id=where,
+            device_id_type=MESH,
+        )
+
+    loads = [
+        pltpu.make_async_copy(a, b, w_sem.at[k])
+        for k, (a, b) in enumerate(((wg_hbm, wg), (wu_hbm, wu), (wd_hbm, wd)))
+    ]
+    for load in loads:
+        load.start()
+
+    barrier = pltpu.get_barrier_semaphore()
+    everyone = [device(f, s, 1 - c, c)]
+    for step in range(1, n):
+        everyone += [device(f + step, s, core, c) for core in range(2)]
+        everyone += [device(f, s + step, core, c) for core in range(2)]
+    for where in everyone:
+        pl.semaphore_signal(barrier, inc=1, device_id=where, device_id_type=MESH)
+
+    values = att[...].astype(jnp.float32)
+    factor = lax.rsqrt(jnp.mean(values * values, axis=-1, keepdims=True) + EPSILON)
+    gathered[0] = (values * factor * gain[...]).astype(jnp.bfloat16)
+    metas[0] = meta[...]
+    pl.semaphore_wait(barrier, len(everyone))
+
+    meta_copies = [
+        remote(
+            meta, metas.at[n - k], meta_send.at[k - 1], meta_recv.at[n - k - 1], device(f + k, s, c, c)
+        )
+        for k in range(1, n)
+    ]
+
+    def ag_copy(k, way, u):
+        source = (n - (k - 1)) % n if way == 0 else k - 1
+        target = n - k if way == 0 else k
+        span = pl.ds(u * half_rows, half_rows)
+        return remote(
+            gathered.at[source, span],
+            gathered.at[target, span],
+            ag_send.at[k - 1, way, u],
+            ag_recv.at[k - 1, way, u],
+            device(f + (1 if way == 0 else -1), s, c, c),
+        )
+
+    def exists(k, way, u, short):
+        return 1 <= k <= far and (k != short or u == way)
+
+    for k in range(1, far + 1):
+        for u in range(2):
+            for way in range(2):
+                if not exists(k, way, u, far):
+                    continue
+                if k > 1:
+                    ag_copy(k - 1, way, u).wait_recv()
+                ag_copy(k, way, u).start()
+        if k == 1:
+            for copy in meta_copies:
+                copy.start()
+
+    for copy in meta_copies:
+        copy.wait_recv()
+    row = lax.broadcasted_iota(jnp.int32, (2 * n, rows), 0)
+    index, core = row >> 1, row & 1
+    reach = (index + 1) >> 1
+    second = (s + jnp.where((index & 1) == 1, reach, -reach) + n) & (n - 1)
+    expert_x = f * (1 - c) + second * c
+    expert_y = second * (1 - c) + f * c
+    expert = ((expert_y * 2 + core) * n + expert_x).astype(jnp.float32)
+    earlier = jnp.where(
+        lax.broadcasted_iota(jnp.int32, (rows, rows), 0)
+        < lax.broadcasted_iota(jnp.int32, (rows, rows), 1),
+        1.0,
+        0.0,
+    ).astype(jnp.bfloat16)
+    for source in range(n):
+        known = metas[source]
+        hit = jnp.zeros((2 * n, rows), jnp.float32)
+        weight = jnp.zeros((2 * n, rows), jnp.float32)
+        for k in range(top):
+            same = known[k : k + 1] == expert
+            hit = jnp.where(same, 1.0, hit)
+            weight = jnp.where(same, known[top + k : top + k + 1], weight)
+        rank = jnp.dot(hit.astype(jnp.bfloat16), earlier, preferred_element_type=jnp.float32)
+        keys[:, source * rows : (source + 1) * rows] = jnp.where(
+            hit > 0.0, rank + float(source * cap), -1.0
+        )
+        routes[:, source * rows : (source + 1) * rows] = weight
+
+    for way in range(2):
+        ag_copy(far - 1, way, 1 - way).wait_recv()
+        ag_copy(far, way, way).wait_recv()
+
+    def offset(index):
+        return lax.div(index + 1, 2) * (2 * lax.rem(index, 2) - 1)
+
+    def out_copy(index, core):
+        return remote(
+            outbox.at[index, core],
+            inbox.at[index, c],
+            out_send.at[index, core],
+            out_recv.at[index, c],
+            device(f, s + offset(index), core, c),
+        )
+
+    slot = lax.broadcasted_iota(jnp.int32, (block, n * rows), 0).astype(jnp.float32)
+
+    def send_rows(index, carry):
+        picks = jnp.concatenate(
+            [
+                jnp.where(slot == keys[pl.ds(2 * index + core, 1), :], 1.0, 0.0).astype(jnp.bfloat16)
+                for core in range(2)
+            ],
+            axis=0,
+        )
+        picked = jnp.dot(
+            picks, gathered[...].reshape(n * rows, width), preferred_element_type=jnp.float32
+        ).astype(jnp.bfloat16)
+        outbox[index] = picked.reshape(2, block, width)
+
+        @pl.when(index == 0)
+        def _():
+            inbox[0, c] = outbox[0, c]
+            out_copy(0, 1 - c).start()
+
+        @pl.when(index > 0)
+        def _():
+            for core in range(2):
+                out_copy(index, core).start()
+
+        return carry
+
+    lax.fori_loop(0, n, send_rows, 0)
+
+    narrow = lax.broadcasted_iota(jnp.int32, (block, rows), 0).astype(jnp.float32)
+
+    def weigh(source, carry):
+        span = pl.ds(pl.multiple_of(source * rows, rows), rows)
+        for e in range(2 * n):
+            piece = jnp.where(narrow == keys[e : e + 1, span], routes[e : e + 1, span], 0.0)
+            tall[e * block : (e + 1) * block] = piece
+        whole = tall[...].T
+        rounded = whole.astype(jnp.bfloat16)
+        mix[source, 0:rows] = rounded
+        mix[source, rows : 2 * rows] = (whole - rounded.astype(jnp.float32)).astype(jnp.bfloat16)
+        return carry
+
+    lax.fori_loop(0, n, weigh, 0)
+    for load in loads:
+        load.wait()
+
+    def back_copy(index, core):
+        first = f * (1 - c) + s * c
+        at_x = first
+        at_y = s * (1 - c) + f * c
+        move = offset(index)
+        where = (
+            g,
+            lax.rem(at_y - move * (1 - core) + n, n) * 2 + core,
+            lax.rem(at_x - move * core + n, n),
+        )
+        return remote(
+            results.at[index, core],
+            combined.at[index, c],
+            back_send.at[index, core],
+            back_recv.at[index, c],
+            where,
+        )
+
+    def out_arrival(index, core):
+        return remote(
+            outbox.at[index, core],
+            inbox.at[index, core],
+            out_send.at[index, core],
+            out_recv.at[index, core],
+            device(f, s, 1 - c, c),
+        )
+
+    def back_arrival(index, core):
+        return remote(
+            results.at[index, core],
+            combined.at[index, core],
+            back_send.at[index, core],
+            back_recv.at[index, core],
+            device(f, s, 1 - c, c),
+        )
+
+    hidden_width = wg.shape[1]
+    tile = 256
+
+    def work(b, carry):
+        for j in range(4):
+            index, core = 2 * b + j // 2, j % 2
+
+            @pl.when((index > 0) | (core != c))
+            def _(index=index, core=core):
+                out_arrival(index, core).wait_recv()
+
+        def first(t, inner):
+            span = pl.ds(pl.multiple_of(t * tile, tile), tile)
+            received = inbox[pl.ds(2 * b, 2)].reshape(4 * block, width)
+            gate = jnp.dot(received, wg[:, span], preferred_element_type=jnp.float32)
+            up = jnp.dot(received, wu[:, span], preferred_element_type=jnp.float32)
+            hidden[:, span] = (gate / (1.0 + jnp.exp(-gate)) * up).astype(jnp.bfloat16)
+            return inner
+
+        lax.fori_loop(0, hidden_width // tile, first, 0)
+
+        def second(t, inner):
+            span = pl.ds(pl.multiple_of(t * tile, tile), tile)
+            made = jnp.dot(hidden[...], wd[:, span], preferred_element_type=jnp.float32)
+            results[pl.ds(2 * b, 2), :, :, span] = made.astype(jnp.bfloat16).reshape(
+                2, 2, block, tile
+            )
+            return inner
+
+        lax.fori_loop(0, width // tile, second, 0)
+
+        @pl.when(b == 0)
+        def _():
+            combined[0, c] = results[0, c]
+
+        for j in range(4):
+            index, core = 2 * b + j // 2, j % 2
+
+            @pl.when((index > 0) | (core != c))
+            def _(index=index, core=core):
+                back_copy(index, core).start()
+
+        return carry
+
+    lax.fori_loop(0, n // 2, work, 0)
+
+    def arrive(index, carry):
+        for core in range(2):
+
+            @pl.when((index > 0) | (core != c))
+            def _(core=core):
+                back_arrival(index, core).wait_recv()
+
+        return carry
+
+    lax.fori_loop(0, n, arrive, 0)
+
+    wide = 512
+
+    def weighted(source, place):
+        def piece(t, carry):
+            span = pl.ds(pl.multiple_of(t * wide, wide), wide)
+            both = jnp.dot(
+                mix[source],
+                combined[:, :, :, span].reshape(2 * n * block, wide),
+                preferred_element_type=jnp.float32,
+            )
+            part[place * rows : (place + 1) * rows, span] = both[:rows] + both[rows:]
+            return carry
+
+        lax.fori_loop(0, width // wide, piece, 0)
+
+    def rs_copy(k, way, u):
+        span = pl.ds(u * half_rows, half_rows)
+        return remote(
+            ring_out.at[k - 1, way, span],
+            ring_in.at[k - 1, way, span],
+            rs_send.at[k - 1, way, u],
+            rs_recv.at[k - 1, way, u],
+            device(f + (1 if way == 0 else -1), s, c, c),
+        )
+
+    for k in range(1, far + 1):
+        d = far + 1 - k
+        weighted(d, 0)
+        if k > 1:
+            weighted(n - d, 1)
+        for u in range(2):
+            for way in range(2):
+                if not exists(k, way, u, 1):
+                    continue
+                low, high = u * half_rows, (u + 1) * half_rows
+                base = 0 if k == 1 else way * rows
+                total = part[base + low : base + high]
+                if exists(k - 1, way, u, 1):
+                    rs_copy(k - 1, way, u).wait_recv()
+                    total = total + ring_in[k - 2, way, low:high].astype(jnp.float32)
+                ring_out[k - 1, way, low:high] = total.astype(jnp.bfloat16)
+                rs_copy(k, way, u).start()
+    weighted(0, 0)
+    for u in range(2):
+        low, high = u * half_rows, (u + 1) * half_rows
+        total = part[low:high]
+        for way in range(2):
+            rs_copy(far, way, u).wait_recv()
+            total = total + ring_in[far - 1, way, low:high].astype(jnp.float32)
+        out[low:high] = total.astype(jnp.bfloat16)
+
+    for copy in meta_copies:
+        copy.wait_send()
+    for k in range(1, far + 1):
+        for u in range(2):
+            for way in range(2):
+                if exists(k, way, u, far):
+                    ag_copy(k, way, u).wait_send()
+                if exists(k, way, u, 1):
+                    rs_copy(k, way, u).wait_send()
+
+    def leave(index, carry):
+        for core in range(2):
+
+            @pl.when((index > 0) | (core != c))
+            def _(core=core):
+                out_copy(index, core).wait_send()
+                back_copy(index, core).wait_send()
+
+        return carry
+
+    lax.fori_loop(0, n, leave, 0)
+
+
+def expert_branch(attended, post_gain, w_gate, w_up, w_down, expert_ids, gate_weights):
+    rows, width = attended.shape
+    top = expert_ids.shape[1]
+    inner = w_gate.shape[2]
+    n = lax.axis_size("dec")
+    experts = n * lax.axis_size("pre")
+    cap = max(2, rows * top * 5 // (4 * experts))
+    block = n * cap
+    route = gate_weights / jnp.sum(gate_weights, axis=-1, keepdims=True)
+    meta = jnp.concatenate([expert_ids.astype(jnp.float32), route], axis=1).T
+    far = n // 2
+    bf16, f32 = jnp.bfloat16, jnp.float32
+    dma = pltpu.SemaphoreType.DMA
+    vmem = pl.BlockSpec(memory_space=pltpu.VMEM)
+    hbm = pl.BlockSpec(memory_space=pl.ANY)
+    return pl.pallas_call(
+        functools.partial(moe_kernel, n, cap),
+        out_shape=jax.ShapeDtypeStruct((rows, width), bf16),
+        in_specs=[vmem] * 3 + [hbm] * 3,
+        out_specs=vmem,
+        scratch_shapes=[
+            pltpu.VMEM((width, inner), bf16),
+            pltpu.VMEM((width, inner), bf16),
+            pltpu.VMEM((inner, width), bf16),
+            pltpu.VMEM((n, rows, width), bf16),
+            pltpu.VMEM((n, 2 * top, rows), f32),
+            pltpu.VMEM((2 * n, n * rows), f32),
+            pltpu.VMEM((2 * n, n * rows), f32),
+            pltpu.VMEM((n, 2, block, width), bf16),
+            pltpu.VMEM((n, 2, block, width), bf16),
+            pltpu.VMEM((4 * block, inner), bf16),
+            pltpu.VMEM((n, 2, block, width), bf16),
+            pltpu.VMEM((n, 2, block, width), bf16),
+            pltpu.VMEM((n, 2 * rows, 2 * n * block), bf16),
+            pltpu.VMEM((2 * n * block, rows), f32),
+            pltpu.VMEM((2 * rows, width), f32),
+            pltpu.VMEM((far, 2, rows, width), bf16),
+            pltpu.VMEM((far, 2, rows, width), bf16),
+            dma((3,)),
+            dma((far, 2, 2)),
+            dma((far, 2, 2)),
+            dma((n - 1,)),
+            dma((n - 1,)),
+            dma((n, 2)),
+            dma((n, 2)),
+            dma((n, 2)),
+            dma((n, 2)),
+            dma((far, 2, 2)),
+            dma((far, 2, 2)),
+        ],
+        compiler_params=pltpu.CompilerParams(
+            collective_id=0, has_side_effects=True, vmem_limit_bytes=64 * 1024 * 1024 - 65536
+        ),
+        name="expert_branch",
+    )(
+        attended,
+        post_gain.reshape(1, width),
+        meta,
+        w_gate.reshape(width, inner),
+        w_up.reshape(width, inner),
+        w_down.reshape(inner, width),
+    )
 
 
 def body(
@@ -174,51 +606,8 @@
     cache = jnp.concatenate(
         [keys.reshape(local_tokens, half), projected[:, half:].astype(jnp.bfloat16)], axis=1
     )
-    normed = norm_rows(attended, post_gain).astype(jnp.bfloat16)
-    experts_here = w_gate.shape[0]
-    pre_count = lax.axis_size("pre")
-    experts_all = experts_here * pre_count * lax.axis_size("dec")
-    top_count = expert_ids.shape[1]
-    capacity = max(2, local_tokens * top_count * 5 // (4 * experts_all))
-    flat_ids = expert_ids.reshape(-1)
-    picks = (flat_ids[:, None] == jnp.arange(experts_all, dtype=jnp.int32)[None, :]).astype(
-        jnp.int32
-    )
-    before = jnp.sum((jnp.cumsum(picks, axis=0) - 1) * picks, axis=1)
-    slot_index = flat_ids * capacity + before
-    source_rows = jnp.repeat(jnp.arange(local_tokens, dtype=jnp.int32), top_count)
-    outgoing = (
-        jnp.zeros((experts_all * capacity, model_width), jnp.bfloat16)
-        .at[slot_index]
-        .set(normed[source_rows])
-    )
-
-    def run_experts(received):
-        count = received.shape[1]
-        grouped = received.reshape(-1, experts_here, count, model_width)
-        gate_part = jnp.einsum(
-            "necd,edf->necf", grouped, w_gate, preferred_element_type=jnp.float32
-        )
-        up_part = jnp.einsum("necd,edf->necf", grouped, w_up, preferred_element_type=jnp.float32)
-        hidden = (jax.nn.silu(gate_part) * up_part).astype(jnp.bfloat16)
-        result = jnp.einsum(
-            "necf,efd->necd", hidden, w_down, preferred_element_type=jnp.float32
-        ).astype(jnp.bfloat16)
-        return result.reshape(-1, count, model_width)
-
-    def serve(received):
-        return lax.all_to_all(
-            run_experts(received), ("pre", "dec"), split_axis=0, concat_axis=0, tiled=True
-        )
-
-    returned = grouped_exchange(
-        outgoing.reshape(experts_all, capacity, model_width), ("pre", "dec"), 0, 0, serve, 1, 1
-    )
-    rows_back = returned.reshape(experts_all * capacity, model_width)
-    picked = rows_back[slot_index].reshape(local_tokens, top_count, model_width).astype(jnp.float32)
-    route = gate_weights / jnp.sum(gate_weights, axis=-1, keepdims=True)
-    moe_out = jnp.einsum("tk,tkd->td", route, picked, precision=lax.Precision.HIGHEST).astype(
-        jnp.bfloat16
+    moe_out = expert_branch(
+        attended, post_gain, w_gate, w_up, w_down, expert_ids, gate_weights
     )
     device = lax.axis_index("dec")
     owners = assignment[:, 0]

time: 604 us -> 298 us (0.49)
  the two profiles are of different devices: /device:TPU:520 before, /device:TPU:513 now
where the time goes in v1:
time: 298 us; the launch traced here: 293 us
  Pallas kernels  194 us (65%)
  waiting for transfers between devices  61.9 us (21%)
  between operations  14.4 us (5%)
  other arithmetic  11.3 us (4%)
  local copies, waits for them, and re-layouts  7.1 us (2%)
  matrix products  4.69 us (2%)
    pallas_call x1, Pallas kernels, expert_branch(): pl.pallas_call(functools.partial(moe_kernel, n, cap), out_shape=jax.Shape...  194 us
    all_gather x1, waiting for transfers between devices, body(): lax.all_gather(kv_weight, 'pre', axis=0, tiled=True)  61.1 us
  transfers between devices with their start and end apart: 2, of which 1 were waited for; matrix products, arithmetic and copies ran while one was open for 3% of the time, Pallas kernels for 66%

profile of v1, /device:TPU:513, one launch (start us, length us, event | category | flops | bytes accessed | tf_op | source)
XLA Modules:
  0.0 293.5 jit_solution(6005151383659970702)
XLA Ops:
  7.2 0.7 all-gather.5.cloned.1.call-update
  8.0 0.8 reduce-window.17
  8.9 0.1 convert_reduce_fusion
  9.0 0.7 select_reduce_fusion
  9.8 0.1 reshape.189
  9.9 0.1 dynamic_slice.44
  9.9 1.2 fusion.5
  11.2 61.1 %all-gather.5.cloned.1.call-done = bf16[2048,1024]{1,0:T(8,128)(2,1)} async-done(((bf16[128,1024]{1,0:T(8,128)(2,1)}), bf16[2048,1024]{1,0:T(8,128)(2,1)}) %all-gather.5.cloned.1.call-update) | async-done | bytes 4194320 | tf_op jit(solution)/shard_map/all_gather | solution.py:599
  72.3 3.1 %fusion.8 = f32[128,1024]{1,0:T(8,128)S(1)} fusion(bf16[2048,1024]{1,0:T(8,128)(2,1)} %all-gather.5.cloned.1.call-done, bf16[128,2048]{1,0:T(8,128)(2,1)} %param.18, f32[2048]{0:T(1024)} %param.20, f32[128]{0:T(128)S(1)} %add_rsqrt_fusion.1), kind=kOutput, calls=%fused_computation.18 | convolution fusion | flops 537919488 | bytes 5251584 | tf_op jit(solution)/shard_map/dot_general | solution.py:597
  75.6 0.1 reshape.190
  75.7 0.2 multiply_reduce_fusion
  75.9 0.2 fusion.12
  76.1 0.3 fusion.35
  76.5 0.2 fusion.15
  76.7 0.3 convolution_bitcast_fusion
  77.0 0.1 reshape.193
  77.1 0.1 max_broadcast_in_dim.12
  77.2 0.7 maximum_bitcast_fusion
  78.0 0.6 bitcast_convert_fusion
  78.6 0.6 copy.56
  79.2 0.6 compare_bitcast_fusion
  79.8 0.7 reduce-window.16
  80.5 0.6 maximum_bitcast_fusion.1.meta
  81.1 193.8 %expert_branch.1 = bf16[128,2048]{1,0:T(8,128)(2,1)} custom-call(bf16[128,2048]{1,0:T(8,128)(2,1)} %att.1, f32[1,2048]{1,0:T(1,128)} %bitcast.76, f32[16,128]{1,0:T(8,128)} %maximum_bitcast_fusion.1.meta, bf16[2048,768]{1,0:T(8,128)(2,1)} %bitcast.68, bf16[2048,768]{1,0:T(8,128)(2,1)} %bitcast.69, bf16[768,2048]{1,0:T(8,128)(2,1)} %bitcast.70), custom_call_target="tpu_custom_call" | custom-call | tf_op jit(solution)/shard_map/expert_branch/pallas_call | solution.py:527
  274.9 0.6 add_bitcast_fusion
  275.6 0.8 select_reduce_fusion.1
  276.4 0.8 fusion.27
  277.2 1.0 fusion.19
  278.2 0.8 fusion.33
  279.1 0.2 reshape_reshape.10
  279.3 0.2 reshape_reshape.9
  279.5 0.8 fusion.34
  280.2 0.1 squeeze.43
  280.3 0.1 squeeze.44
  280.4 1.4 slice.44
  281.8 0.9 dynamic_slice.50
  282.7 1.6 while.19
  282.7 0.2 fusion.40
  283.0 0.2 fusion.40
  283.2 0.2 fusion.40
  283.4 0.2 fusion.40
  283.7 0.2 fusion.40
  283.9 0.2 fusion.40
  284.1 0.2 fusion.40
  284.4 0.2 fusion.21
  284.6 0.6 gather_fusion
  285.1 0.7 broadcast_select_fusion
  285.8 0.8 copy.97
  (45 shorter events, 0.8 us)
Async XLA Ops:
  7.2 65.1 %all-gather.5.cloned.1.call-start = ((), (), s32[]{:S(2)}) async-start(), calls=%async_computation | async-start | bytes 4456448 | tf_op jit(solution)/shard_map/all_gather | solution.py:599
  8.0 270.2 %all-gather.7.cloned.1.call-start = ((), (), s32[]{:S(2)}) async-start(), calls=%async_computation.1 | async-start | bytes 1216512 | tf_op jit(solution)/shard_map/all_gather | solution.py:31
  11.2 64.7 %copy-start.6 = (f32[128]{0:T(128)S(1)}, f32[128]{0:T(128)}, u32[]{:S(2)}) copy-start(f32[128]{0:T(128)} %param.23) | copy-start | bytes 1540
  11.2 64.9 %copy-start.7 = (bf16[8,4096]{1,0:T(8,128)(2,1)S(1)}, bf16[8,4096]{1,0:T(8,128)(2,1)}, u32[]{:S(2)}) copy-start(bf16[8,4096]{1,0:T(8,128)(2,1)} %param.32) | copy-start | bytes 196612
  75.4 2.5 copy-start.3
  75.5 3.7 %copy-start.5 = (s32[8,1]{0,1:T(1,128)S(1)}, s32[8,1]{0,1:T(1,128)}, u32[]{:S(2)}) copy-start(s32[8,1]{0,1:T(1,128)} %param.31) | copy-start | bytes 100
  75.5 5.0 %copy-start.4 = (s32[128,8]{0,1:T(8,128)S(1)}, s32[128,8]{0,1:T(8,128)}, u32[]{:S(2)}) copy-start(s32[128,8]{0,1:T(8,128)} %param.27) | copy-start | bytes 12292
  75.5 5.0 %copy-start.2 = (f32[128,8]{0,1:T(8,128)S(1)}, f32[128,8]{0,1:T(8,128)}, u32[]{:S(2)}) copy-start(f32[128,8]{0,1:T(8,128)} %param.28) | copy-start | bytes 12292
  274.9 9.4 %copy-start.1 = (f32[8,4,128]{2,1,0:T(4,128)S(1)}, f32[8,4,128]{2,1,0:T(4,128)}, u32[]{:S(2)}) copy-start(f32[8,4,128]{2,1,0:T(4,128)} %copy.56) | copy-start | bytes 49156
  280.3 5.5 %copy-start = (bf16[128,2048]{1,0:T(8,128)(2,1)S(1)}, bf16[128,2048]{1,0:T(8,128)(2,1)}, u32[]{:S(2)}) copy-start(bf16[128,2048]{1,0:T(8,128)(2,1)} %expert_branch.1) | copy-start | bytes 1572868
Sparse Core Ops, SparseCore 0:
  9.9 62.4 all-gather.4
  78.1 35.0 all-gather.6

commit v2 on v1

v2 whole, which is shorter than its diff:
```python
import functools

import jax
import jax.numpy as jnp
from jax import lax
from jax.experimental import pallas as pl
from jax.experimental.pallas import tpu as pltpu
from jax.sharding import PartitionSpec as P

MESH = pl.DeviceIdType.MESH

H = 32
KVH = 4
HD = 128
PAGE = 16
RCAP = 3


EPSILON = 1e-06
FLOOR_SCORE = -1e30


def norm_rows(values, scales):
    values = values.astype(jnp.float32)
    factor = lax.rsqrt(jnp.mean(values * values, axis=-1, keepdims=True) + EPSILON)
    return values * factor * scales


def step_kernel(
    n,
    cap,
    att,
    gain,
    ids,
    gates,
    toks,
    in_gain,
    kvw,
    key_gain,
    pages,
    counts,
    owners,
    queries,
    fresh,
    wg_hbm,
    wu_hbm,
    wd_hbm,
    out,
    dec_out,
    wg,
    wu,
    wd,
    gathered,
    metas,
    keys,
    routes,
    outbox,
    inbox,
    hidden,
    results,
    combined,
    mix,
    tall,
    part,
    ring_out,
    ring_in,
    normed_in,
    kv_all,
    projected,
    mixes,
    peaks,
    states,
    arrived,
    w_sem,
    ag_send,
    ag_recv,
    meta_send,
    meta_recv,
    out_send,
    out_recv,
    back_send,
    back_recv,
    rs_send,
    rs_recv,
    kv_send,
    kv_recv,
    pair_send,
    pair_recv,
    dec_send,
    dec_recv,
):
    rows, width = att.shape
    top = ids.shape[0]
    block = n * cap
    half_rows = rows // 2
    far = n // 2
    last = n - 1
    main = 8
    extra = cap - main
    tail = n * main
    g, pre, x = lax.axis_index("groups"), lax.axis_index("pre"), lax.axis_index("dec")
    y, c = lax.div(pre, 2), lax.rem(pre, 2)
    f = x * (1 - c) + y * c
    s = y * (1 - c) + x * c

    def device(first, second, core, orient):
        first, second = lax.rem(first + 2 * n, n), lax.rem(second + 2 * n, n)
        at_x = first * (1 - orient) + second * orient
        at_y = second * (1 - orient) + first * orient
        return (g, at_y * 2 + core, at_x)

    def remote(source, target, send, recv, where):
        return pltpu.make_async_remote_copy(
            src_ref=source,
            dst_ref=target,
            send_sem=send,
            recv_sem=recv,
            device_id=where,
            device_id_type=MESH,
        )

    loads = [
        pltpu.make_async_copy(a, b, w_sem.at[k])
        for k, (a, b) in enumerate(((wg_hbm, wg), (wu_hbm, wu), (wd_hbm, wd)))
    ]
    for load in loads:
        load.start()

    barrier = pltpu.get_barrier_semaphore()
    everyone = [device(f, s, 1 - c, c)]
    for step in range(1, n):
        everyone += [device(f + step, s, core, c) for core in range(2)]
        everyone += [device(f, s + step, core, c) for core in range(2)]
    for where in everyone:
        pl.semaphore_signal(barrier, inc=1, device_id=where, device_id_type=MESH)

    gathered[0] = norm_rows(att[...], gain[...]).astype(jnp.bfloat16)
    share_of = gates[...] / jnp.sum(gates[...], axis=0, keepdims=True)
    metas[0, 0:top] = ids[...].astype(jnp.float32)
    metas[0, top : 2 * top] = share_of
    pl.semaphore_wait(barrier, len(everyone))

    kv_rows = kvw.shape[0]
    kv_half = kv_rows // 2
    partner = (g, y * 2 + 1 - c, x)

    def kv_copy(k, way):
        span = pl.ds(0, kv_rows) if k < far else pl.ds(way * kv_half, kv_half)
        move = -(k - 1) if way == 0 else k - 1
        block_at = lax.rem(y + move + n, n) * 2 + c
        where = (g, lax.rem(y + (1 if way == 0 else n - 1), n) * 2 + c, x)
        return remote(
            kvw if k == 1 else kv_all.at[block_at, span],
            kv_all.at[block_at, span],
            kv_send.at[k - 1, way],
            kv_recv.at[k - 1, way],
            where,
        )

    def pair_copy(index):
        block_at = lax.rem(y + index, n) * 2 + c
        return remote(
            kvw if index == 0 else kv_all.at[block_at],
            kv_all.at[block_at],
            pair_send.at[index],
            pair_recv.at[index],
            partner,
        )

    def kv_step(k):
        if k > 1:
            for way in range(2):
                kv_copy(k - 1, way).wait_recv()
        if k <= far:
            for way in range(2):
                kv_copy(k, way).start()
        if k == 1:
            pair_copy(0).start()
        elif k <= far:
            pair_copy(n - (k - 1)).start()
            pair_copy(k - 1).start()
        else:
            pair_copy(far).start()

    meta_copies = [
        remote(
            metas.at[0], metas.at[n - k], meta_send.at[k - 1], meta_recv.at[n - k - 1], device(f + k, s, c, c)
        )
        for k in range(1, n)
    ]

    def ag_copy(k, way, u):
        source = (n - (k - 1)) % n if way == 0 else k - 1
        target = n - k if way == 0 else k
        span = pl.ds(u * half_rows, half_rows)
        return remote(
            gathered.at[source, span],
            gathered.at[target, span],
            ag_send.at[k - 1, way, u],
            ag_recv.at[k - 1, way, u],
            device(f + (1 if way == 0 else -1), s, c, c),
        )

    def exists(k, way, u, short):
        return 1 <= k <= far and (k != short or u == way)

    for k in range(1, far + 1):
        for u in range(2):
            for way in range(2):
                if not exists(k, way, u, far):
                    continue
                if k > 1:
                    ag_copy(k - 1, way, u).wait_recv()
                ag_copy(k, way, u).start()
        if k == 1:
            for copy in meta_copies:
                copy.start()

        @pl.when(c == 0)
        def _(k=k):
            kv_step(k)


    kv_all[pre] = kvw[...]
    normed_in[...] = norm_rows(toks[...], in_gain[...]).astype(jnp.bfloat16)

    for copy in meta_copies:
        copy.wait_recv()
    row = lax.broadcasted_iota(jnp.int32, (2 * n, rows), 0)
    index, core = row >> 1, row & 1
    reach = jnp.where(index == last, 0, (index >> 1) + 1)
    second = (s + jnp.where((index & 1) == 1, -reach, reach) + n) & (n - 1)
    expert_x = f * (1 - c) + second * c
    expert_y = second * (1 - c) + f * c
    expert = ((expert_y * 2 + core) * n + expert_x).astype(jnp.float32)
    earlier = jnp.where(
        lax.broadcasted_iota(jnp.int32, (rows, rows), 0)
        < lax.broadcasted_iota(jnp.int32, (rows, rows), 1),
        1.0,
        0.0,
    ).astype(jnp.bfloat16)
    for source in range(n):
        known = metas[source]
        hit = jnp.zeros((2 * n, rows), jnp.float32)
        weight = jnp.zeros((2 * n, rows), jnp.float32)
        for k in range(top):
            same = known[k : k + 1] == expert
            hit = jnp.where(same, 1.0, hit)
            weight = jnp.where(same, known[top + k : top + k + 1], weight)
        rank = jnp.dot(hit.astype(jnp.bfloat16), earlier, preferred_element_type=jnp.float32)
        keys[:, source * rows : (source + 1) * rows] = jnp.where(
            hit > 0.0,
            jnp.where(
                rank < main, rank + float(source * main), rank + float(tail + source * extra - main)
            ),
            -1.0,
        )
        routes[:, source * rows : (source + 1) * rows] = weight

    for way in range(2):
        ag_copy(far - 1, way, 1 - way).wait_recv()
        ag_copy(far, way, way).wait_recv()

    def kv_turn(core, k):
        @pl.when(c == core)
        def _():
            kv_step(k)

    kv_turn(0, far + 1)
    kv_turn(1, 1)

    def offset(index):
        return (lax.div(index, 2) + 1) * (1 - 2 * lax.rem(index, 2)) * (1 - lax.div(index, n - 1))

    def out_copy(index, core):
        return remote(
            outbox.at[index, core],
            inbox.at[index, c],
            out_send.at[index, core],
            out_recv.at[index, c],
            device(f, s + offset(index), core, c),
        )

    slot = lax.broadcasted_iota(jnp.int32, (block, n * rows), 0).astype(jnp.float32)

    def send_rows(index, carry):
        picks = jnp.concatenate(
            [
                jnp.where(slot == keys[pl.ds(2 * index + core, 1), :], 1.0, 0.0).astype(jnp.bfloat16)
                for core in range(2)
            ],
            axis=0,
        )
        picked = jnp.dot(
            picks, gathered[...].reshape(n * rows, width), preferred_element_type=jnp.float32
        ).astype(jnp.bfloat16)
        outbox[index] = picked.reshape(2, block, width)

        @pl.when(index == last)
        def _():
            inbox[last, c] = outbox[last, c]
            out_copy(last, 1 - c).start()

        @pl.when(index < last)
        def _():
            for core in range(2):
                out_copy(index, core).start()

        return carry

    lax.fori_loop(0, n, send_rows, 0)
    kv_turn(1, 2)

    pair = 2 * main
    line = lax.broadcasted_iota(jnp.int32, (2 * pair, rows), 0)

    def weigh(source, carry):
        span = pl.ds(pl.multiple_of(source * rows, rows), rows)
        narrow = (
            line + jnp.where(line < pair, lax.div(source, 2) * pair, tail - pair)
        ).astype(jnp.float32)
        for e in range(2 * n):
            piece = jnp.where(narrow == keys[e : e + 1, span], routes[e : e + 1, span], 0.0)
            tall[e * pair : (e + 1) * pair] = piece[:pair]
            tall[(2 * n + e) * pair : (2 * n + e + 1) * pair] = piece[pair:]
        whole = tall[...].T
        rounded = whole.astype(jnp.bfloat16)
        mix[source, 0:rows] = rounded
        mix[source, rows : 2 * rows] = (whole - rounded.astype(jnp.float32)).astype(jnp.bfloat16)
        return carry

    lax.fori_loop(0, n, weigh, 0)
    kv_turn(1, 3)
    for load in loads:
        load.wait()

    def back_copy(index, core):
        first = f * (1 - c) + s * c
        at_x = first
        at_y = s * (1 - c) + f * c
        move = offset(index)
        where = (
            g,
            lax.rem(at_y - move * (1 - core) + n, n) * 2 + core,
            lax.rem(at_x - move * core + n, n),
        )
        return remote(
            results.at[index, core],
            combined.at[index, c],
            back_send.at[index, core],
            back_recv.at[index, c],
            where,
        )

    def out_arrival(index, core):
        return remote(
            outbox.at[index, core],
            inbox.at[index, core],
            out_send.at[index, core],
            out_recv.at[index, core],
            device(f, s, 1 - c, c),
        )

    def back_arrival(index, core):
        return remote(
            results.at[index, core],
            combined.at[index, core],
            back_send.at[index, core],
            back_recv.at[index, core],
            device(f, s, 1 - c, c),
        )

    hidden_width = wg.shape[1]
    tile = 256

    def work(b, carry):
        for j in range(4):
            index, core = 2 * b + j // 2, j % 2

            @pl.when((index < last) | (core != c))
            def _(index=index, core=core):
                out_arrival(index, core).wait_recv()

        def first(t, inner):
            span = pl.ds(pl.multiple_of(t * tile, tile), tile)
            received = inbox[pl.ds(2 * b, 2)].reshape(4 * block, width)
            gate = jnp.dot(received, wg[:, span], preferred_element_type=jnp.float32)
            up = jnp.dot(received, wu[:, span], preferred_element_type=jnp.float32)
            hidden[:, span] = (gate / (1.0 + jnp.exp(-gate)) * up).astype(jnp.bfloat16)
            return inner

        lax.fori_loop(0, hidden_width // tile, first, 0)

        def second(t, inner):
            span = pl.ds(pl.multiple_of(t * tile, tile), tile)
            made = jnp.dot(hidden[...], wd[:, span], preferred_element_type=jnp.float32)
            results[pl.ds(2 * b, 2), :, :, span] = made.astype(jnp.bfloat16).reshape(
                2, 2, block, tile
            )
            return inner

        lax.fori_loop(0, width // tile, second, 0)

        @pl.when(b == n // 2 - 1)
        def _():
            combined[last, c] = results[last, c]

        for j in range(4):
            index, core = 2 * b + j // 2, j % 2

            @pl.when((index < last) | (core != c))
            def _(index=index, core=core):
                back_copy(index, core).start()

        return carry

    work(0, 0)
    kv_turn(1, 4)
    work(1, 0)
    kv_turn(1, 5)
    for index in range(n):
        pair_copy(index).wait_recv()

    kv_tile = 256

    def project(t, carry):
        span = pl.ds(pl.multiple_of(t * kv_tile, kv_tile), kv_tile)
        projected[:, span] = jnp.dot(
            normed_in[...],
            kv_all[:, :, span].reshape(width, kv_tile),
            preferred_element_type=jnp.float32,
        )
        return carry

    kv_width = kvw.shape[1]
    lax.fori_loop(0, kv_width // kv_tile, project, 0)

    requests = owners.shape[1]
    group = H // KVH
    lane = lax.broadcasted_iota(jnp.int32, (1, rows), 1)
    page_of = x * (rows // PAGE) + lax.div(lane, PAGE)
    place = jnp.zeros((1, rows), jnp.int32)
    for p in range(pages.shape[1]):
        place = jnp.where(page_of == pages[0, p], p, place)
    owner_of = jnp.zeros((1, rows), jnp.int32)
    end = 0
    slots = []
    for r in range(requests):
        end = end + counts[0, r]
        owner_of = owner_of + jnp.where(place >= end, 1, 0)
        order = 0
        for other in range(r):
            order = order + jnp.where(owners[0, other] == owners[0, r], 1, 0)
        slots.append(owners[0, r] * RCAP + order)
    members = owner_of == (
        lax.div(lax.broadcasted_iota(jnp.int32, (requests * group, rows), 0), group)
    )
    asked = queries[...].astype(jnp.float32)
    by_head = asked.reshape(requests, KVH, group, HD)
    half = KVH * HD
    left = lax.broadcasted_iota(jnp.int32, (requests * group, HD), 1) < HD // 2
    for head in range(KVH):
        key = norm_rows(projected[:, head * HD : (head + 1) * HD], key_gain[...]).astype(
            jnp.bfloat16
        )
        value = projected[:, half + head * HD : half + (head + 1) * HD].astype(jnp.bfloat16)
        wanted = by_head[:, head].reshape(requests * group, HD).astype(jnp.bfloat16)
        scores = lax.dot_general(
            wanted, key, (((1,), (1,)), ((), ())), preferred_element_type=jnp.float32
        ) * HD ** (-0.5)
        scores = jnp.where(members, scores, FLOOR_SCORE)
        peak = jnp.max(scores, axis=-1, keepdims=True)
        weights = jnp.where(members, jnp.exp(scores - peak), 0.0)
        upper = weights.astype(jnp.bfloat16)
        lower = (weights - upper.astype(jnp.float32)).astype(jnp.bfloat16)
        mixed = jnp.dot(upper, value, preferred_element_type=jnp.float32) + jnp.dot(
            lower, value, preferred_element_type=jnp.float32
        )
        sums = jnp.sum(weights, axis=-1, keepdims=True)
        mixes[:, head] = mixed.reshape(requests, group, HD)
        peaks[:, head] = jnp.where(left, peak, sums).reshape(requests, group, HD)

    lines = RCAP * H
    diagonal = lax.broadcasted_iota(jnp.int32, (lines, HD), 0) == lax.broadcasted_iota(
        jnp.int32, (lines, HD), 1
    )

    def chosen(device_at, source):
        found = []
        for q in range(RCAP):
            value = 0.0
            for r in range(requests):
                here = jnp.where(slots[r] == device_at * RCAP + q, 1.0, 0.0)
                value = value + here * source(r)
            found.append(value)
        return jnp.concatenate(found, axis=0)

    def dec_copy(device_at):
        return remote(
            states.at[device_at],
            arrived.at[x],
            dec_send.at[device_at],
            dec_recv.at[x],
            (g, pre, device_at),
        )

    def dec_arrival(device_at):
        return remote(
            states.at[device_at],
            arrived.at[device_at],
            dec_send.at[device_at],
            dec_recv.at[device_at],
            (g, pre, device_at),
        )

    def share(step, carry):
        device_at = lax.rem(x + step, n)
        states[device_at, 0:lines] = chosen(device_at, lambda r: mixes[r].reshape(H, HD))
        both = chosen(device_at, lambda r: peaks[r].reshape(H, HD))
        top_row = jnp.sum(jnp.where(diagonal, both[:, 0:1], 0.0), axis=0, keepdims=True)
        sum_row = jnp.sum(jnp.where(diagonal, both[:, HD - 1 : HD], 0.0), axis=0, keepdims=True)
        states[device_at, lines : lines + 8] = jnp.concatenate(
            [top_row, sum_row, jnp.zeros((6, HD), jnp.float32)], axis=0
        )

        @pl.when(step > 0)
        def _():
            dec_copy(device_at).start()

        @pl.when(step == 0)
        def _():
            arrived[x] = states[x]

        return carry

    lax.fori_loop(0, n, share, 0)
    lax.fori_loop(n // 4, n // 2, work, 0)

    for step in range(1, n):
        dec_arrival(lax.rem(x + step, n)).wait_recv()

    def column(line):
        return jnp.sum(jnp.where(diagonal, line, 0.0), axis=1, keepdims=True)

    highest = arrived[0, lines : lines + 1]
    for source in range(1, n):
        highest = jnp.maximum(highest, arrived[source, lines : lines + 1])
    total = jnp.zeros((1, HD), jnp.float32)
    blended = jnp.zeros((lines, HD), jnp.float32)
    for source in range(n):
        scale = jnp.exp(arrived[source, lines : lines + 1] - highest)
        total = total + arrived[source, lines + 1 : lines + 2] * scale
        blended = blended + arrived[source, 0:lines] * column(scale)
    new = fresh[...].astype(jnp.float32)

    def spread(r, base):
        return jnp.concatenate(
            [
                jnp.broadcast_to(
                    new[r : r + 1, base + head * HD : base + (head + 1) * HD], (group, HD)
                )
                for head in range(KVH)
            ],
            axis=0,
        )

    my_queries = chosen(x, lambda r: asked[r * H : (r + 1) * H])
    my_keys = chosen(x, lambda r: spread(r, 0))
    my_values = chosen(x, lambda r: spread(r, half))
    live = chosen(x, lambda r: jnp.ones((H, HD), jnp.float32))
    own = jnp.sum(my_queries * my_keys, axis=-1, keepdims=True) * HD ** (-0.5)
    old_top = column(highest)
    final = jnp.maximum(old_top, own)
    old_part = jnp.exp(old_top - final)
    new_part = jnp.exp(own - final)
    made = (blended * old_part + new_part * my_values) / (column(total) * old_part + new_part)
    dec_out[...] = jnp.where(live > 0.0, made, 0.0).astype(jnp.bfloat16)

    def arrive(index, carry):
        for core in range(2):

            @pl.when((index < last) | (core != c))
            def _(core=core):
                back_arrival(index, core).wait_recv()

        return carry

    lax.fori_loop(0, n, arrive, 0)

    wide = 512

    def weighted(source, place):
        def piece(t, carry):
            span = pl.ds(pl.multiple_of(t * wide, wide), wide)
            low = source // 2 * pair
            both = jnp.dot(
                mix[source, :, 0 : 2 * n * pair],
                combined[:, :, low : low + pair, span].reshape(2 * n * pair, wide),
                preferred_element_type=jnp.float32,
            ) + jnp.dot(
                mix[source, :, 2 * n * pair :],
                combined[:, :, tail : tail + pair, span].reshape(2 * n * pair, wide),
                preferred_element_type=jnp.float32,
            )
            part[place * rows : (place + 1) * rows, span] = both[:rows] + both[rows:]
            return carry

        lax.fori_loop(0, width // wide, piece, 0)

    def rs_copy(k, way, u):
        span = pl.ds(u * half_rows, half_rows)
        return remote(
            ring_out.at[k - 1, way, span],
            ring_in.at[k - 1, way, span],
            rs_send.at[k - 1, way, u],
            rs_recv.at[k - 1, way, u],
            device(f + (1 if way == 0 else -1), s, c, c),
        )

    for k in range(1, far + 1):
        d = far + 1 - k
        weighted(d, 0)
        if k > 1:
            weighted(n - d, 1)
        for u in range(2):
            for way in range(2):
                if not exists(k, way, u, 1):
                    continue
                low, high = u * half_rows, (u + 1) * half_rows
                base = 0 if k == 1 else way * rows
                total = part[base + low : base + high]
                if exists(k - 1, way, u, 1):
                    rs_copy(k - 1, way, u).wait_recv()
                    total = total + ring_in[k - 2, way, low:high].astype(jnp.float32)
                ring_out[k - 1, way, low:high] = total.astype(jnp.bfloat16)
                rs_copy(k, way, u).start()
    weighted(0, 0)
    for u in range(2):
        low, high = u * half_rows, (u + 1) * half_rows
        total = part[low:high]
        for way in range(2):
            rs_copy(far, way, u).wait_recv()
            total = total + ring_in[far - 1, way, low:high].astype(jnp.float32)
        out[low:high] = total.astype(jnp.bfloat16)

    for copy in meta_copies:
        copy.wait_send()
    for k in range(1, far + 1):
        for u in range(2):
            for way in range(2):
                if exists(k, way, u, far):
                    ag_copy(k, way, u).wait_send()
                if exists(k, way, u, 1):
                    rs_copy(k, way, u).wait_send()

    def leave(index, carry):
        for core in range(2):

            @pl.when((index < last) | (core != c))
            def _(core=core):
                out_copy(index, core).wait_send()
                back_copy(index, core).wait_send()

        return carry

    lax.fori_loop(0, n, leave, 0)
    for k in range(1, far + 1):
        for way in range(2):
            kv_copy(k, way).wait_send()
    for index in range(n):
        pair_copy(index).wait_send()
    for step in range(1, n):
        dec_copy(lax.rem(x + step, n)).wait_send()


def body(
    tokens,
    attended,
    input_gain,
    post_gain,
    kv_weight,
    key_gain,
    w_gate,
    w_up,
    w_down,
    expert_ids,
    gate_weights,
    page_list,
    lengths,
    assignment,
    query,
    new_kv,
):
    rows, width = attended.shape
    top = expert_ids.shape[1]
    inner = w_gate.shape[2]
    n = lax.axis_size("dec")
    experts = n * lax.axis_size("pre")
    cap = max(2, rows * top * 5 // (4 * experts))
    block = n * cap
    far = n // 2
    bf16, f32 = jnp.bfloat16, jnp.float32
    dma = pltpu.SemaphoreType.DMA
    vmem = pl.BlockSpec(memory_space=pltpu.VMEM)
    hbm = pl.BlockSpec(memory_space=pl.ANY)
    smem = pl.BlockSpec(memory_space=pltpu.SMEM)
    requests = assignment.shape[0]
    lines = RCAP * H
    kv_rows, kv_width = kv_weight.shape
    moe_out, decode_out = pl.pallas_call(
        functools.partial(step_kernel, n, cap),
        out_shape=(
            jax.ShapeDtypeStruct((rows, width), bf16),
            jax.ShapeDtypeStruct((lines, HD), bf16),
        ),
        in_specs=[vmem] * 8 + [smem] * 3 + [vmem] * 2 + [hbm] * 3,
        out_specs=(vmem, vmem),
        scratch_shapes=[
            pltpu.VMEM((width, inner), bf16),
            pltpu.VMEM((width, inner), bf16),
            pltpu.VMEM((inner, width), bf16),
            pltpu.VMEM((n, rows, width), bf16),
            pltpu.VMEM((n, 2 * top, rows), f32),
            pltpu.VMEM((2 * n, n * rows), f32),
            pltpu.VMEM((2 * n, n * rows), f32),
            pltpu.VMEM((n, 2, block, width), bf16),
            pltpu.VMEM((n, 2, block, width), bf16),
            pltpu.VMEM((4 * block, inner), bf16),
            pltpu.VMEM((n, 2, block, width), bf16),
            pltpu.VMEM((n, 2, block, width), bf16),
            pltpu.VMEM((n, 2 * rows, 64 * n), bf16),
            pltpu.VMEM((64 * n, rows), f32),
            pltpu.VMEM((2 * rows, width), f32),
            pltpu.VMEM((far, 2, rows, width), bf16),
            pltpu.VMEM((far, 2, rows, width), bf16),
            pltpu.VMEM((rows, width), bf16),
            pltpu.VMEM((2 * n, kv_rows, kv_width), bf16),
            pltpu.VMEM((rows, kv_width), f32),
            pltpu.VMEM((requests, KVH, H // KVH, HD), f32),
            pltpu.VMEM((requests, KVH, H // KVH, HD), f32),
            pltpu.VMEM((n, lines + 8, HD), f32),
            pltpu.VMEM((n, lines + 8, HD), f32),
            dma((3,)),
            dma((far, 2, 2)),
            dma((far, 2, 2)),
            dma((n - 1,)),
            dma((n - 1,)),
            dma((n, 2)),
            dma((n, 2)),
            dma((n, 2)),
            dma((n, 2)),
            dma((far, 2, 2)),
            dma((far, 2, 2)),
            dma((far, 2)),
            dma((far, 2)),
            dma((n,)),
            dma((n,)),
            dma((n,)),
            dma((n,)),
        ],
        compiler_params=pltpu.CompilerParams(
            collective_id=0, has_side_effects=True, vmem_limit_bytes=64 * 1024 * 1024 - 65536
        ),
        name="whole_step",
    )(
        attended,
        post_gain.reshape(1, width),
        expert_ids.T,
        gate_weights.T,
        tokens,
        input_gain.reshape(1, width),
        kv_weight,
        key_gain.reshape(1, HD),
        page_list,
        lengths,
        assignment.T,
        query.reshape(requests * H, HD),
        new_kv,
        w_gate.reshape(width, inner),
        w_up.reshape(width, inner),
        w_down.reshape(inner, width),
    )
    return moe_out, decode_out.reshape(RCAP, H * HD)


def solution(mesh):
    in_specs = (
        P(("groups", "pre", "dec"), None),
        P(("groups", "pre", "dec"), None),
        P(),
        P(),
        P("pre", None),
        P(),
        P(("pre", "dec"), None, None),
        P(("pre", "dec"), None, None),
        P(("pre", "dec"), None, None),
        P(("groups", "pre", "dec"), None),
        P(("groups", "pre", "dec"), None),
        P(("groups", "pre"), None),
        P(("groups", "pre"), None),
        P(("groups", "pre"), None),
        P(("groups", "pre"), None),
        P(("groups", "pre"), None),
    )
    out_specs = (P(("groups", "pre", "dec"), None), P(("groups", "pre", "dec"), None))
    return jax.shard_map(body, mesh=mesh, in_specs=in_specs, out_specs=out_specs, check_vma=False)
```

time: 298 us -> 218 us (0.73); the launches traced: 293 us -> 217 us
  waiting for transfers between devices: 61.9 us -> 0 us
  Pallas kernels: 194 us -> 212 us
  between operations: 14.4 us -> 0.64 us
  other arithmetic: 11.3 us -> 0 us
  matrix products: 4.69 us -> 0 us
    all_gather x2 -> x0, waiting for transfers between devices: 61.1 us -> none  [the longest x1 61.1 us: body(): lax.all_gather(kv_weight, 'pre', axis=0, tiled=True)]
    pallas_call x1, Pallas kernels: 194 us -> 212 us  [body(): pl.pallas_call(functools.partial(step_kernel, n, cap), out_shape=(jax.Sha...]
    dot_general x4 -> x0, matrix products: 4.69 us -> none  [the longest x1 3.12 us: body(): jnp.dot(normed_in, lax.all_gather(kv_weight, 'pre', axis=0, tiled=True),...]
    reduce_sum x7 -> x0, other arithmetic: 3.3 us -> none  [the longest x2 1.44 us: norm_rows(): jnp.mean(values * values, axis=-1, keepdims=True) + EPSILON]
  transfers between devices with their start and end apart: 2 -> 0, of which waited for: 1 -> 0; matrix products, arithmetic and copies ran while one was open for 3% -> 0% of each run, Pallas kernels for 66% -> 0%
where the time goes in v2:
time: 218 us; the launch traced here: 217 us
  Pallas kernels  212 us (97%)
  local copies, waits for them, and re-layouts  4.75 us (2%)
    pallas_call x1, Pallas kernels, body(): pl.pallas_call(functools.partial(step_kernel, n, cap), out_shape=(jax.Sha...  212 us

profile of v2, /device:TPU:513, one launch (start us, length us, event | category | flops | bytes accessed | tf_op | source)
XLA Modules:
  0.0 217.4 jit_solution(5518225597588491401)
XLA Ops:
  0.6 1.5 reshape.31.queries
  2.1 212.0 %whole_step.1 = (bf16[128,2048]{1,0:T(8,128)(2,1)}, bf16[96,128]{1,0:T(8,128)(2,1)}) custom-call(bf16[128,2048]{1,0:T(8,128)(2,1)} %att.1, f32[1,2048]{1,0:T(1,128)} %bitcast.12, s32[8,128]{1,0:T(8,128)} %bitcast.14, f32[8,128]{1,0:T(8,128)} %bitcast.15, bf16[128,2048]{1,0:T(8,128)(2,1)} %toks.1, f32[1,2048]{1,0:T(1,128)} %bitcast.13, ...), custom_call_target="tpu_custom_call" | custom-call | tf_op jit(solution)/shard_map/whole_step/pallas_call | solution.py:710
  214.2 1.4 reshape.35
  215.5 1.9 copy.19

commit v3 on v2

--- a/solution.py
+++ b/solution.py
@@ -24,6 +24,12 @@
     values = values.astype(jnp.float32)
     factor = lax.rsqrt(jnp.mean(values * values, axis=-1, keepdims=True) + EPSILON)
     return values * factor * scales
+
+
+def place_results(moe, dec, moe_out, dec_out):
+    moe_out[...] = moe[...]
+    for h in range(H):
+        dec_out[:, h * HD : (h + 1) * HD] = dec[pl.ds(h, RCAP, stride=H), :].astype(jnp.bfloat16)
 
 
 def step_kernel(
@@ -64,6 +70,7 @@
     part,
     ring_out,
     ring_in,
+    asked,
     normed_in,
     kv_all,
     projected,
@@ -220,6 +227,10 @@
         def _(k=k):
             kv_step(k)
 
+    @pl.when(c == 1)
+    def _():
+        kv_step(1)
+
 
     kv_all[pre] = kvw[...]
     normed_in[...] = norm_rows(toks[...], in_gain[...]).astype(jnp.bfloat16)
@@ -267,7 +278,6 @@
             kv_step(k)
 
     kv_turn(0, far + 1)
-    kv_turn(1, 1)
 
     def offset(index):
         return (lax.div(index, 2) + 1) * (1 - 2 * lax.rem(index, 2)) * (1 - lax.div(index, n - 1))
@@ -455,8 +465,11 @@
     members = owner_of == (
         lax.div(lax.broadcasted_iota(jnp.int32, (requests * group, rows), 0), group)
     )
-    asked = queries[...].astype(jnp.float32)
-    by_head = asked.reshape(requests, KVH, group, HD)
+    for h in range(H):
+        asked[pl.ds(h, requests, stride=H), :] = queries[:, h * HD : (h + 1) * HD].astype(
+            jnp.float32
+        )
+    by_head = asked[...].reshape(requests, KVH, group, HD)
     half = KVH * HD
     left = lax.broadcasted_iota(jnp.int32, (requests * group, HD), 1) < HD // 2
     for head in range(KVH):
@@ -574,7 +587,7 @@
     old_part = jnp.exp(old_top - final)
     new_part = jnp.exp(own - final)
     made = (blended * old_part + new_part * my_values) / (column(total) * old_part + new_part)
-    dec_out[...] = jnp.where(live > 0.0, made, 0.0).astype(jnp.bfloat16)
+    dec_out[...] = jnp.where(live > 0.0, made, 0.0)
 
     def arrive(index, carry):
         for core in range(2):
@@ -711,7 +724,7 @@
         functools.partial(step_kernel, n, cap),
         out_shape=(
             jax.ShapeDtypeStruct((rows, width), bf16),
-            jax.ShapeDtypeStruct((lines, HD), bf16),
+            jax.ShapeDtypeStruct((lines, HD), f32),
         ),
         in_specs=[vmem] * 8 + [smem] * 3 + [vmem] * 2 + [hbm] * 3,
         out_specs=(vmem, vmem),
@@ -733,6 +746,7 @@
             pltpu.VMEM((2 * rows, width), f32),
             pltpu.VMEM((far, 2, rows, width), bf16),
             pltpu.VMEM((far, 2, rows, width), bf16),
+            pltpu.VMEM((requests * H, HD), f32),
             pltpu.VMEM((rows, width), bf16),
             pltpu.VMEM((2 * n, kv_rows, kv_width), bf16),
             pltpu.VMEM((rows, kv_width), f32),
@@ -774,13 +788,23 @@
         page_list,
         lengths,
         assignment.T,
-        query.reshape(requests * H, HD),
+        query,
         new_kv,
         w_gate.reshape(width, inner),
         w_up.reshape(width, inner),
         w_down.reshape(inner, width),
     )
-    return moe_out, decode_out.reshape(RCAP, H * HD)
+    return pl.pallas_call(
+        place_results,
+        out_shape=(
+            jax.ShapeDtypeStruct((rows, width), bf16),
+            jax.ShapeDtypeStruct((RCAP, H * HD), bf16),
+        ),
+        in_specs=[vmem] * 2,
+        out_specs=(vmem, vmem),
+        compiler_params=pltpu.CompilerParams(vmem_limit_bytes=16 * 1024 * 1024),
+        name="place_results",
+    )(moe_out, decode_out)
 
 
 def solution(mesh):

time: 218 us -> 216 us (level)
  local copies, waits for them, and re-layouts: 4.75 us -> 1.83 us
    reshape x2 -> x0, local copies, waits for them, and re-layouts: 2.87 us -> none  [the longest x1 1.5 us: body(): query.reshape(requests * H, HD)]
where the time goes in v3:
time: 216 us
  Pallas kernels  213 us (99%)
    pallas_call x1, Pallas kernels, body(): pl.pallas_call(functools.partial(step_kernel, n, cap), out_shape=(jax.Sha...  213 us

profile of v3, /device:TPU:513, one launch (start us, length us, event | category | flops | bytes accessed | tf_op | source)
XLA Modules:
  0.0 215.9 jit_solution(6720479820763423661)
XLA Ops:
  0.6 212.6 %whole_step.1 = (bf16[128,2048]{1,0:T(8,128)(2,1)}, f32[96,128]{1,0:T(8,128)}) custom-call(bf16[128,2048]{1,0:T(8,128)(2,1)} %att.1, f32[1,2048]{1,0:T(1,128)} %bitcast.12, s32[8,128]{1,0:T(8,128)} %bitcast.14, f32[8,128]{1,0:T(8,128)} %bitcast.15, bf16[128,2048]{1,0:T(8,128)(2,1)} %toks.1, f32[1,2048]{1,0:T(1,128)} %bitcast.13, bf16[128,1024]{1,0:T(8,128)(2,1)} %kvw.1, ...), custom_call_target="tpu_custom_call" | custom-call | tf_op jit(solution)/shard_map/whole_step/pallas_call | solution.py:723
  213.2 0.0 copy-start
  213.2 1.0 copy-done
  214.3 0.0 copy-start.1
  214.3 0.8 copy-done.1
  215.1 0.9 place_results.1
Async XLA Ops:
  213.2 1.0 copy-start
  214.3 0.8 copy-start.1

commit v4 on v3

--- a/solution.py
+++ b/solution.py
@@ -26,10 +26,15 @@
     return values * factor * scales
 
 
-def place_results(moe, dec, moe_out, dec_out):
-    moe_out[...] = moe[...]
+def place_results(moe, dec, moe_out, dec_out, held, sems):
+    whole = pltpu.make_async_copy(moe, moe_out, sems.at[0])
+    small = pltpu.make_async_copy(dec, held, sems.at[1])
+    whole.start()
+    small.start()
+    small.wait()
     for h in range(H):
-        dec_out[:, h * HD : (h + 1) * HD] = dec[pl.ds(h, RCAP, stride=H), :].astype(jnp.bfloat16)
+        dec_out[:, h * HD : (h + 1) * HD] = held[pl.ds(h, RCAP, stride=H), :].astype(jnp.bfloat16)
+    whole.wait()
 
 
 def step_kernel(
@@ -635,8 +640,9 @@
         weighted(d, 0)
         if k > 1:
             weighted(n - d, 1)
-        for u in range(2):
+        for turn in range(2):
             for way in range(2):
+                u = way if turn else 1 - way
                 if not exists(k, way, u, 1):
                     continue
                 low, high = u * half_rows, (u + 1) * half_rows
@@ -800,9 +806,10 @@
             jax.ShapeDtypeStruct((rows, width), bf16),
             jax.ShapeDtypeStruct((RCAP, H * HD), bf16),
         ),
-        in_specs=[vmem] * 2,
+        in_specs=[pl.BlockSpec(memory_space=pltpu.HBM)] * 2,
         out_specs=(vmem, vmem),
-        compiler_params=pltpu.CompilerParams(vmem_limit_bytes=16 * 1024 * 1024),
+        scratch_shapes=[pltpu.VMEM((lines, HD), f32), dma((2,))],
+        compiler_params=pltpu.CompilerParams(vmem_limit_bytes=64 * 1024 * 1024 - 65536),
         name="place_results",
     )(moe_out, decode_out)
 

time: 216 us -> 213 us (0.986)
  no operation moved by 1% of the time
where the time goes in v4:
time: 213 us
  Pallas kernels  212 us (100%)
    pallas_call x1, Pallas kernels, body(): pl.pallas_call(functools.partial(step_kernel, n, cap), out_shape=(jax.Sha...  211 us

profile of v4, /device:TPU:513, one launch (start us, length us, event | category | flops | bytes accessed | tf_op | source)
XLA Modules:
  0.0 213.1 jit_solution(3210940547017246708)
XLA Ops:
  0.6 210.6 %whole_step.1 = (bf16[128,2048]{1,0:T(8,128)(2,1)}, f32[96,128]{1,0:T(8,128)}) custom-call(bf16[128,2048]{1,0:T(8,128)(2,1)} %att.1, f32[1,2048]{1,0:T(1,128)} %bitcast.12, s32[8,128]{1,0:T(8,128)} %bitcast.14, f32[8,128]{1,0:T(8,128)} %bitcast.15, bf16[128,2048]{1,0:T(8,128)(2,1)} %toks.1, f32[1,2048]{1,0:T(1,128)} %bitcast.13, bf16[128,1024]{1,0:T(8,128)(2,1)} %kvw.1, ...), custom_call_target="tpu_custom_call" | custom-call | tf_op jit(solution)/shard_map/whole_step/pallas_call | solution.py:729
  211.2 1.9 place_results.1
